TPU v7x, 32 devices: a whole 2x2x4 slice. The times are simulated.
32 devices in a mesh: blk: 4 (over y, x), grp: 8 (over z, core).
Axes of the slice: x: 2, y: 2, z: 4, core: 2. Of those that a mesh axis runs over, the one named last changes fastest.
Arguments:
- queries: bfloat16 [32, 32, 128], P('blk', 'grp'), may hold values from -3 to 3
- token_counts: int32 [32], P('blk'), may hold values from 8 to 32
- pages: bfloat16 [32, 1024, 128], P(('blk', 'grp')), may hold values from -6 to 6
- patch_counts: int32 [32], P(('blk', 'grp')), may hold values from 512 to 1024
- labels: int32 [32, 32], P(None, ('blk', 'grp')), may hold values 0 or 1
Outputs:
- query_grad: float32 [32, 32, 128], P('blk', 'grp')
- page_grad: float32 [32, 1024, 128], P(('blk', 'grp'))
- page_loss: float32 [32], P(('blk', 'grp'))
All inputs are finite; a program needn't handle non-finite values. No bound on the sum of `labels` on one device may be relied on, other than what follows from the above.
Results may differ from a plain program's by a relative error of at most 0.018.
Values may be sent and summed in bfloat16 or wider, within the bound.
A program may use at most 64 MiB of HBM per device.

v0:
```python
import functools
import math

import jax
import jax.numpy as jnp
from jax import lax
from jax.experimental import pallas as pl
from jax.experimental.pallas import tpu as pltpu
from jax.sharding import PartitionSpec as P

align_sharpness = 4.0
logit_scale = 2.0
logit_bias = -5.0
masked = -1e30
exp2_scale = align_sharpness * math.log2(math.e)
MESH = pl.DeviceIdType.MESH
patch_tile = 128


def partner(position, step, size):
    if size & (size - 1):
        return lax.rem(position + step, size)
    result = 0
    bit = 1
    while bit < size:
        here = lax.rem(position // bit, 2)
        flip = (step // bit) % 2
        result = result + (1 - here if flip else here) * bit
        bit *= 2
    return result


def source(position, step, size):
    if size & (size - 1):
        return lax.rem(position + size - step, size)
    return partner(position, step, size)


def fold(value):
    return value.reshape(-1, 8, value.shape[1])


def kernel(
    blocks, groups, block_queries, slice_tokens,
    query_in, count_in, page_in, patch_count_in, label_in,
    query_grad_ref, page_grad_ref, loss_ref,
    query_ref, count_ref, page_ref, patch_count_ref, label_ref,
    held, count_rows, bias, scores, exponents, grads, own_term,
    part_send, part_recv, sum_send, sum_recv,
    column_send, column_recv, row_send, row_recv, count_send, count_recv,
    part_send_sem, part_recv_sem, sum_send_sem, sum_recv_sem, load_sem,
):
    blk = lax.axis_index("blk")
    grp = lax.axis_index("grp")
    patches, width = page_ref.shape
    rows = block_queries * slice_tokens
    block_rows = rows * groups
    total_queries = blocks * block_queries
    tiles = [pl.ds(start, patch_tile) for start in range(0, patches, patch_tile)]

    barrier = pltpu.get_barrier_semaphore()
    for step in range(1, groups):
        pl.semaphore_signal(
            barrier, inc=1, device_id=(blk, partner(grp, step, groups)), device_id_type=MESH
        )
    for step in range(blocks - 1, 0, -1):
        pl.semaphore_signal(
            barrier, inc=1, device_id=(partner(blk, step, blocks), grp), device_id_type=MESH
        )

    loads = [
        pltpu.make_async_copy(src, dst, load_sem.at[index])
        for index, (src, dst) in enumerate((
            (query_in, query_ref), (count_in, count_ref), (page_in, page_ref),
            (patch_count_in, patch_count_ref), (label_in, label_ref),
        ))
    ]
    for load in loads:
        load.start()

    lane = lax.broadcasted_iota(jnp.int32, (1, block_rows), 1)
    query_row = lax.rem(lane // slice_tokens, block_queries)
    token_row = lane // rows * slice_tokens + lax.rem(lane, slice_tokens)
    loads[0].wait()
    loads[1].wait()
    counts = jnp.zeros((1, block_rows), jnp.float32)
    for index in range(block_queries):
        counts = jnp.where(query_row == index, count_ref[index].astype(jnp.float32), counts)
    count_rows[blk] = counts
    held[blk, grp] = query_ref[...]

    pl.semaphore_wait(barrier, groups - 1 + blocks - 1)

    def remote(src, dst, send, recv, device):
        pltpu.make_async_remote_copy(
            src_ref=src, dst_ref=dst, send_sem=send, recv_sem=recv,
            device_id=device, device_id_type=MESH,
        ).start()

    def settle(ref, sem):
        pltpu.make_async_copy(ref, ref, sem).wait()

    for step in range(groups - 1, 0, -1):
        remote(
            query_ref, held.at[blk, grp], column_send, column_recv.at[grp],
            (blk, partner(grp, step, groups)),
        )
    for step in range(blocks - 1, 0, -1):
        other = partner(blk, step, blocks)
        remote(query_ref, held.at[blk, grp], row_send, row_recv.at[blk], (other, grp))
        remote(count_rows.at[blk], count_rows.at[blk], count_send, count_recv.at[blk], (other, grp))

    for load in loads[2:]:
        load.wait()
    patch_count = patch_count_ref[0]
    for index, tile in enumerate(tiles):
        patch = index * patch_tile + lax.broadcasted_iota(jnp.int32, (patch_tile, width), 0)
        bias[tile, :] = jnp.where(patch < patch_count, 0.0, masked)
    same_query = (
        lax.rem(lax.broadcasted_iota(jnp.int32, (block_rows, block_rows), 0) // slice_tokens, block_queries)
        == lax.rem(lax.broadcasted_iota(jnp.int32, (block_rows, block_rows), 1) // slice_tokens, block_queries)
    )
    same_query = jnp.where(same_query, 1.0, 0.0).astype(jnp.bfloat16)

    for step in range(1, groups):
        origin = source(grp, step, groups)
        settle(held.at[blk, origin], column_recv.at[origin])
        for hop in range(blocks - 1, 0, -1):
            remote(
                held.at[blk, origin], held.at[blk, origin], row_send, row_recv.at[blk],
                (partner(blk, hop, blocks), grp),
            )

    def block_terms(origin):
        query_rows = held[origin].reshape(block_rows, width)
        row_max = None
        for tile in tiles:
            tile_scores = lax.dot_general(
                page_ref[tile, :], query_rows, (((1,), (1,)), ((), ())),
                preferred_element_type=jnp.float32,
            )
            tile_bias = bias[tile, :]
            tile_scores = tile_scores + jnp.concatenate([tile_bias] * (block_rows // width), axis=1)
            scores[tile, :] = tile_scores
            tile_max = jnp.max(fold(tile_scores), axis=0)
            row_max = tile_max if row_max is None else jnp.maximum(row_max, tile_max)
        row_max = jnp.max(row_max, axis=0, keepdims=True)
        total = jnp.zeros((8, block_rows), jnp.float32)
        moment = jnp.zeros((8, block_rows), jnp.float32)
        for tile in tiles:
            shifted = scores[tile, :] - row_max
            exponent = jnp.exp2(shifted * exp2_scale)
            scores[tile, :] = shifted
            exponents[tile, :] = exponent
            total = total + jnp.sum(fold(exponent), axis=0)
            moment = moment + jnp.sum(fold(exponent * shifted), axis=0)
        total = jnp.sum(total, axis=0, keepdims=True)
        shifted_score = jnp.sum(moment, axis=0, keepdims=True) / total
        token_score = shifted_score + row_max

        count_row = count_rows[origin]
        live = token_row.astype(jnp.float32) < count_row
        remaining = jnp.where(live, token_score, 0.0)
        sublane = lax.broadcasted_iota(jnp.int32, (16, block_rows), 0)
        pieces = jnp.zeros((16, block_rows), jnp.float32)
        for index in range(3):
            piece = remaining.astype(jnp.bfloat16).astype(jnp.float32)
            pieces = jnp.where(sublane == index, piece, pieces)
            remaining = remaining - piece
        pair_sum = jnp.sum(
            jnp.dot(
                pieces.astype(jnp.bfloat16), same_query, preferred_element_type=jnp.float32
            ),
            axis=0, keepdims=True,
        )
        pair_score = pair_sum / count_row
        label_row = jnp.zeros((1, block_rows), jnp.float32)
        for index in range(block_queries):
            label = label_ref[0, origin * block_queries + index].astype(jnp.float32)
            label_row = jnp.where(query_row == index, label, label_row)
        label_sign = 2.0 * label_row - 1.0
        signed = -label_sign * (logit_scale * pair_score + logit_bias)
        decay = jnp.exp(-jnp.abs(signed))
        softplus = jnp.maximum(signed, 0.0) + jnp.log1p(decay)
        sigmoid = jnp.where(signed >= 0.0, 1.0, decay) / (1.0 + decay)
        loss_row = jnp.where(token_row == 0, softplus, 0.0)
        token_grad = jnp.where(live, -label_sign * logit_scale * sigmoid / count_row, 0.0) / total
        slope = token_grad * align_sharpness
        offset = token_grad * (1.0 - align_sharpness * shifted_score)
        for tile in tiles:
            tile_grad = exponents[tile, :] * (offset + slope * scores[tile, :])
            grads[origin, tile, :] = tile_grad.astype(jnp.bfloat16)
        query_term = lax.dot_general(
            grads[origin], page_ref[...], (((0,), (0,)), ((), ())),
            preferred_element_type=jnp.float32,
        )
        return query_term, loss_row

    own, loss_row = block_terms(blk)
    own_term[...] = own.reshape(groups, rows, width)

    for step in range(blocks - 1, 0, -1):
        origin = source(blk, step, blocks)
        settle(held.at[origin], row_recv.at[origin])
        settle(count_rows.at[origin], count_recv.at[origin])
        query_term, loss_term = block_terms(origin)
        loss_row = loss_row + loss_term
        part_send[origin] = query_term.astype(jnp.bfloat16).reshape(groups, rows, width)
        remote(
            part_send.at[origin], part_recv.at[blk], part_send_sem, part_recv_sem.at[blk],
            (origin, grp),
        )

    def page_term(tile):
        result = jnp.dot(
            grads[0, tile, :], held[0].reshape(block_rows, width), preferred_element_type=jnp.float32
        )
        for index in range(1, blocks):
            result = result + jnp.dot(
                grads[index, tile, :], held[index].reshape(block_rows, width),
                preferred_element_type=jnp.float32,
            )
        page_grad_ref[tile, :] = result

    half = len(tiles) // 2
    for tile in tiles[:half]:
        page_term(tile)

    block_sum = own_term[...]
    for step in range(blocks - 1, 0, -1):
        origin = source(blk, step, blocks)
        settle(part_recv.at[origin], part_recv_sem.at[origin])
        block_sum = block_sum + part_recv[origin].astype(jnp.float32)
    own_term[...] = block_sum
    sum_send[...] = block_sum.astype(jnp.bfloat16)
    for step in range(groups - 1, 0, -1):
        target = partner(grp, step, groups)
        remote(
            sum_send.at[target], sum_recv.at[step - 1], sum_send_sem, sum_recv_sem, (blk, target)
        )
    for tile in tiles[half:]:
        page_term(tile)
    loss_ref[0] = jnp.sum(loss_row) / jnp.float32(total_queries)

    settle(sum_recv, sum_recv_sem)
    result = own_term[grp]
    for step in range(1, groups):
        result = result + sum_recv[step - 1].astype(jnp.float32)
    query_grad_ref[...] = result

    settle(held.at[0, pl.ds(0, groups - 1)], column_send)
    settle(held.at[pl.ds(0, blocks - 1)], row_send)
    settle(count_rows.at[pl.ds(0, blocks - 1)], count_send)
    settle(part_send.at[pl.ds(0, blocks - 1)], part_send_sem)
    settle(sum_send.at[pl.ds(0, groups - 1)], sum_send_sem)


def write_out(query_grad_in, page_grad_in, loss_in, query_grad_ref, page_grad_ref, loss_ref, sems):
    copies = [
        pltpu.make_async_copy(page_grad_in, page_grad_ref, sems.at[0]),
        pltpu.make_async_copy(query_grad_in, query_grad_ref, sems.at[1]),
        pltpu.make_async_copy(loss_in, loss_ref, sems.at[2]),
    ]
    for copy in copies:
        copy.start()
    for copy in copies:
        copy.wait()


def local(queries, token_counts, pages, patch_counts, labels):
    blocks = lax.axis_size("blk")
    groups = lax.axis_size("grp")
    block_queries, slice_tokens, width = queries.shape
    patches = pages.shape[1]
    rows = block_queries * slice_tokens
    block_rows = rows * groups
    vmem = pl.BlockSpec(memory_space=pltpu.VMEM)
    smem = pl.BlockSpec(memory_space=pltpu.SMEM)
    anywhere = pl.BlockSpec(memory_space=pl.ANY)
    dma = pltpu.SemaphoreType.DMA
    query_grad, page_grad, page_loss = pl.pallas_call(
        functools.partial(kernel, blocks, groups, block_queries, slice_tokens),
        out_shape=(
            pltpu.VMEM((rows, width), jnp.float32),
            pltpu.VMEM((patches, width), jnp.float32),
            pltpu.SMEM((1,), jnp.float32),
        ),
        in_specs=[anywhere] * 5,
        out_specs=(vmem, vmem, smem),
        scratch_shapes=[
            pltpu.VMEM((rows, width), jnp.bfloat16),
            pltpu.SMEM(token_counts.shape, jnp.int32),
            pltpu.VMEM((patches, width), jnp.bfloat16),
            pltpu.SMEM((1,), jnp.int32),
            pltpu.SMEM((1, labels.shape[0]), jnp.int32),
            pltpu.VMEM((blocks, groups, rows, width), jnp.bfloat16),
            pltpu.VMEM((blocks, 1, block_rows), jnp.float32),
            pltpu.VMEM((patches, width), jnp.float32),
            pltpu.VMEM((patches, block_rows), jnp.float32),
            pltpu.VMEM((patches, block_rows), jnp.float32),
            pltpu.VMEM((blocks, patches, block_rows), jnp.bfloat16),
            pltpu.VMEM((groups, rows, width), jnp.float32),
            pltpu.VMEM((blocks, groups, rows, width), jnp.bfloat16),
            pltpu.VMEM((blocks, groups, rows, width), jnp.bfloat16),
            pltpu.VMEM((groups, rows, width), jnp.bfloat16),
            pltpu.VMEM((groups - 1, rows, width), jnp.bfloat16),
            dma, dma((groups,)), dma, dma((blocks,)), dma, dma((blocks,)),
            dma, dma((blocks,)), dma, dma, dma((5,)),
        ],
        compiler_params=pltpu.CompilerParams(
            collective_id=0, has_side_effects=True, vmem_limit_bytes=60 * 1024 * 1024
        ),
        name="late_interaction",
    )(queries.reshape(rows, width), token_counts, pages[0], patch_counts, labels.T)
    query_grad, page_grad, page_loss = pl.pallas_call(
        write_out,
        out_shape=(
            jax.ShapeDtypeStruct((rows, width), jnp.float32),
            jax.ShapeDtypeStruct((patches, width), jnp.float32),
            jax.ShapeDtypeStruct((1,), jnp.float32),
        ),
        in_specs=[anywhere] * 3,
        out_specs=(anywhere,) * 3,
        scratch_shapes=[dma((3,))],
        compiler_params=pltpu.CompilerParams(vmem_limit_bytes=1024 * 1024),
        name="write_out",
    )(query_grad, page_grad, page_loss)
    return query_grad.reshape(queries.shape), page_grad[None], page_loss


def solution(mesh):
    in_specs = (
        P("blk", "grp", None),
        P("blk"),
        P(("blk", "grp"), None, None),
        P(("blk", "grp")),
        P(None, ("blk", "grp")),
    )
    out_specs = (P("blk", "grp", None), P(("blk", "grp"), None, None), P(("blk", "grp")))
    return jax.shard_map(local, mesh=mesh, in_specs=in_specs, out_specs=out_specs, check_vma=False)
```

profile of v0, /device:TPU:0, one launch (start us, length us, event | category | flops | bytes accessed | tf_op | source)
XLA Modules:
  0.0 25.8 jit_solution(5467220532268101644)
XLA Ops:
  1.3 23.7 %late_interaction.1 = (f32[32,128]{1,0:T(8,128)S(1)}, f32[1024,128]{1,0:T(8,128)S(1)}, f32[1]{0:T(128)S(4)}) custom-call(bf16[32,128]{1,0:T(8,128)(2,1)} %bitcast.6, s32[8]{0:T(128)} %count_in.1, bf16[1024,128]{1,0:T(8,128)(2,1)} %bitcast.5, s32[1]{0:T(128)S(6)} %copy.8.patch_count_in, s32[1,32]{1,0:T(1,128)} %bitcast.7), custom_call_target="tpu_custom_call" | custom-call | tf_op jit(solution)/shard_map/late_interaction/pallas_call | solution.py:281
  25.0 0.8 %write_out.1 = (f32[32,128]{1,0:T(8,128)}, f32[1024,128]{1,0:T(8,128)}, f32[1]{0:T(128)}) custom-call(f32[32,128]{1,0:T(8,128)S(1)} %get-tuple-element.9.query_grad_in, f32[1024,128]{1,0:T(8,128)S(1)} %get-tuple-element.10.page_grad_in, f32[1]{0:T(128)S(4)} %get-tuple-element.11.loss_in), custom_call_target="tpu_custom_call" | custom-call | tf_op jit(solution)/shard_map/write_out/pallas_call | solution.py:315
where the time goes:
time: 26 us; the launch traced here: 25.8 us
  Pallas kernels  24.5 us (94%)
  between operations  1.29 us (5%)
    pallas_call x1, Pallas kernels, local(): pl.pallas_call(functools.partial(kernel, blocks, groups, block_queries, s...  23.7 us
    pallas_call x1, Pallas kernels, local(): pl.pallas_call(write_out, out_shape=(jax.ShapeDtypeStruct((rows, width),...  0.83 us

commit v1 on v0

v1 whole, which is shorter than its diff:
```python
import functools
import math

import jax
import jax.numpy as jnp
from jax import lax
from jax.experimental import pallas as pl
from jax.experimental.pallas import tpu as pltpu
from jax.sharding import PartitionSpec as P

align_sharpness = 4.0
logit_scale = 2.0
logit_bias = -5.0
masked = -1e30
exp2_scale = align_sharpness * math.log2(math.e)
MESH = pl.DeviceIdType.MESH
patch_tile = 256


def partner(position, step, size):
    if size & (size - 1):
        return lax.rem(position + step, size)
    result = 0
    bit = 1
    while bit < size:
        here = lax.rem(position // bit, 2)
        flip = (step // bit) % 2
        result = result + (1 - here if flip else here) * bit
        bit *= 2
    return result


def source(position, step, size):
    if size & (size - 1):
        return lax.rem(position + size - step, size)
    return partner(position, step, size)


def fold(value):
    return value.reshape(-1, 8, value.shape[1])


def kernel(
    blocks, groups, half_queries, slice_tokens,
    query_in, count_in, page_in, patch_count_in, label_in,
    query_grad_ref, page_grad_ref, loss_ref,
    count_ref, page_ref, page_turned, patch_count_ref, label_ref,
    held, query_rows, count_rows, label_rows, extra_rows, bias,
    shifted_ref, exponent_ref, grads, own_term,
    part_send, part_recv, page_send, page_recv, loss_send, loss_recv,
    column_send, column_recv, row_send, row_recv, count_send, count_recv,
    mate_send, mate_recv, near_send, far_send, part_recv_sem,
    page_send_sem, page_recv_sem, loss_send_sem, loss_recv_sem, load_sem,
):
    blk = lax.axis_index("blk")
    grp = lax.axis_index("grp")
    half = lax.rem(grp, 2)
    mate = grp + 1 - 2 * half
    _, patches, width = page_ref.shape
    piece = half_queries * slice_tokens
    rows = piece * groups
    free = patches // 2
    total_queries = blocks * half_queries * 2
    tiles = [pl.ds(start, patch_tile) for start in range(0, patches, patch_tile)]
    tile_folds = patch_tile // 8

    barrier = pltpu.get_barrier_semaphore()
    for step in range(1, groups):
        pl.semaphore_signal(
            barrier, inc=1, device_id=(blk, partner(grp, step, groups)), device_id_type=MESH
        )
    for step in range(blocks - 1, 0, -1):
        pl.semaphore_signal(
            barrier, inc=1, device_id=(partner(blk, step, blocks), grp), device_id_type=MESH
        )

    loads = [
        pltpu.make_async_copy(src, dst, load_sem.at[index])
        for index, (src, dst) in enumerate((
            (count_in, count_ref), (label_in, label_ref), (patch_count_in, patch_count_ref),
            (page_in, page_ref.at[0]), (query_in.at[half], held.at[blk, grp]),
        ))
    ]
    for load in loads:
        load.start()

    def remote(src, dst, send, recv, device):
        pltpu.make_async_remote_copy(
            src_ref=src, dst_ref=dst, send_sem=send, recv_sem=recv,
            device_id=device, device_id_type=MESH,
        ).start()

    def settle(ref, sem):
        pltpu.make_async_copy(ref, ref, sem).wait()

    lane = lax.broadcasted_iota(jnp.int32, (1, rows), 1)
    query_row = lax.rem(lane // slice_tokens, half_queries)
    token_row = lane // piece * slice_tokens + lax.rem(lane, slice_tokens)

    def spread(read):
        result = jnp.zeros((1, rows), jnp.float32)
        for index in range(half_queries):
            result = jnp.where(query_row == index, read(index).astype(jnp.float32), result)
        return result

    for load in loads[:3]:
        load.wait()
    count_rows[blk] = spread(lambda index: count_ref[half * half_queries + index])
    for index in range(blocks):
        first = index * half_queries * 2
        label_rows[0, index] = spread(
            lambda query: label_ref[0, first + half * half_queries + query]
        )
        extra_rows[index] = spread(
            lambda query: label_ref[0, first + (1 - half) * half_queries + query]
        )
    patch_count = patch_count_ref[0].astype(jnp.float32)
    extra_rows[blocks] = jnp.full((1, rows), patch_count, jnp.float32)

    pl.semaphore_wait(barrier, groups - 1 + blocks - 1)

    for step in range(groups - 1, 0, -1):
        target = partner(grp, step, groups)
        remote(
            query_in.at[lax.rem(target, 2)], held.at[blk, grp], column_send, column_recv.at[grp],
            (blk, target),
        )
    for step in range(blocks - 1, 0, -1):
        other = partner(blk, step, blocks)
        remote(query_in.at[half], held.at[blk, grp], row_send, row_recv.at[blk], (other, grp))
        remote(count_rows.at[blk], count_rows.at[blk], count_send, count_recv.at[blk], (other, grp))
    remote(page_in, page_ref.at[1], mate_send.at[0], mate_recv.at[0], (blk, mate))
    remote(extra_rows, label_rows.at[1], mate_send.at[1], mate_recv.at[1], (blk, mate))

    patch = (free + lax.broadcasted_iota(jnp.int32, (patches - free, rows), 0)).astype(jnp.float32)
    same_query = (
        lax.rem(lax.broadcasted_iota(jnp.int32, (rows, rows), 0) // slice_tokens, half_queries)
        == lax.rem(lax.broadcasted_iota(jnp.int32, (rows, rows), 1) // slice_tokens, half_queries)
    )
    same_query = jnp.where(same_query, 1.0, 0.0).astype(jnp.bfloat16)
    loads[3].wait()
    bias[0] = jnp.where(patch < patch_count, 0.0, masked)
    page_turned[0] = page_ref[0].T
    part_recv[blk, grp] = jnp.zeros((piece, width), part_recv.dtype)
    loads[4].wait()

    for step in range(1, groups):
        origin = source(grp, step, groups)
        settle(held.at[blk, origin], column_recv.at[origin])
        for hop in range(blocks - 1, 0, -1):
            remote(
                held.at[blk, origin], held.at[blk, origin], row_send, row_recv.at[blk],
                (partner(blk, hop, blocks), grp),
            )

    settle(page_ref.at[1], mate_recv.at[0])
    settle(label_rows.at[1], mate_recv.at[1])
    bias[1] = jnp.where(patch < label_rows[1, blocks], 0.0, masked)
    page_turned[1] = page_ref[1].T

    def softmax_parts(page, queries):
        parts = []
        for index, tile in enumerate(tiles):
            scores = lax.dot_general(
                page_ref[page, tile, :], queries, (((1,), (1,)), ((), ())),
                preferred_element_type=jnp.float32,
            )
            start = index * patch_tile
            if start >= free:
                scores = scores + bias[page, pl.ds(start - free, patch_tile), :]
            scores = fold(scores)
            top = jnp.max(scores, axis=0)
            shifted = scores - top
            exponent = jnp.exp2(shifted * exp2_scale)
            place = pl.ds(index * tile_folds, tile_folds)
            shifted_ref[page, place] = shifted
            exponent_ref[page, place] = exponent
            parts.append((top, jnp.sum(exponent, axis=0), jnp.sum(exponent * shifted, axis=0)))
        return parts

    def pair_terms(page, parts, origin):
        row_max = parts[0][0]
        for top, _, _ in parts[1:]:
            row_max = jnp.maximum(row_max, top)
        row_max = jnp.max(row_max, axis=0, keepdims=True)
        total = jnp.zeros((8, rows), jnp.float32)
        moment = jnp.zeros((8, rows), jnp.float32)
        scaled = []
        for top, part_total, part_moment in parts:
            gap = top - row_max
            scale = jnp.exp2(gap * exp2_scale)
            total = total + scale * part_total
            moment = moment + scale * (part_moment + gap * part_total)
            scaled.append((gap, scale))
        total = jnp.sum(total, axis=0, keepdims=True)
        shifted_score = jnp.sum(moment, axis=0, keepdims=True) / total
        token_score = shifted_score + row_max

        count_row = count_rows[origin]
        live = token_row.astype(jnp.float32) < count_row
        remaining = jnp.where(live, token_score, 0.0)
        sublane = lax.broadcasted_iota(jnp.int32, (16, rows), 0)
        pieces = jnp.zeros((16, rows), jnp.float32)
        for index in range(3):
            value = remaining.astype(jnp.bfloat16).astype(jnp.float32)
            pieces = jnp.where(sublane == index, value, pieces)
            remaining = remaining - value
        pair_sum = jnp.sum(
            jnp.dot(
                pieces.astype(jnp.bfloat16), same_query, preferred_element_type=jnp.float32
            ),
            axis=0, keepdims=True,
        )
        pair_score = pair_sum / count_row
        label_sign = 2.0 * label_rows[page, origin] - 1.0
        signed = -label_sign * (logit_scale * pair_score + logit_bias)
        decay = jnp.exp(-jnp.abs(signed))
        softplus = jnp.maximum(signed, 0.0) + jnp.log1p(decay)
        sigmoid = jnp.where(signed >= 0.0, 1.0, decay) / (1.0 + decay)
        loss_row = jnp.where(token_row == 0, softplus, 0.0)
        token_grad = jnp.where(live, -label_sign * logit_scale * sigmoid / count_row, 0.0) / total
        lines = []
        for gap, scale in scaled:
            slope = scale * token_grad
            lines.append((
                slope * (1.0 + align_sharpness * (gap - shifted_score)), slope * align_sharpness
            ))
        return lines, loss_row

    def block_terms(order, origin):
        queries = held[origin].reshape(rows, width)
        columns = pl.ds(order * rows, rows)
        query_rows[columns, :] = queries
        parts = [softmax_parts(page, queries) for page in range(2)]
        query_term = jnp.zeros((width, rows), jnp.float32)
        losses = []
        for page in range(2):
            lines, loss_row = pair_terms(page, parts[page], origin)
            losses.append(loss_row)
            for index, (offset, slope) in enumerate(lines):
                place = pl.ds(index * tile_folds, tile_folds)
                tile_grad = exponent_ref[page, place] * (offset + slope * shifted_ref[page, place])
                grads[page, tiles[index], columns] = (
                    tile_grad.reshape(patch_tile, rows).astype(jnp.bfloat16)
                )
            query_term = query_term + jnp.dot(
                page_turned[page], grads[page, :, columns], preferred_element_type=jnp.float32
            )
        return query_term.T, losses

    own, losses = block_terms(0, blk)
    own_term[...] = own.reshape(groups, piece, width)
    part_send[blk] = own.astype(jnp.bfloat16).reshape(groups, piece, width)
    for step in range(groups - 1, 0, -1):
        target = partner(grp, step, groups)
        remote(
            part_send.at[blk, target], part_recv.at[blk, grp], near_send, part_recv_sem.at[blk],
            (blk, target),
        )

    for step in range(blocks - 1):
        origin = step + jnp.where(step >= blk, 1, 0)
        settle(held.at[origin], row_recv.at[origin])
        settle(count_rows.at[origin], count_recv.at[origin])
        query_term, block_losses = block_terms(step + 1, origin)
        losses = [first + second for first, second in zip(losses, block_losses)]
        part_send[origin] = query_term.astype(jnp.bfloat16).reshape(groups, piece, width)
        for target in range(groups):
            remote(
                part_send.at[origin, target], part_recv.at[blk, grp], far_send,
                part_recv_sem.at[blk], (origin, target),
            )

    loss_send[...] = losses[1]
    remote(loss_send, loss_recv, loss_send_sem, loss_recv_sem, (blk, mate))
    for index, tile in enumerate(tiles):
        page_send[tile, :] = jnp.dot(
            grads[1, tile, :], query_rows[...], preferred_element_type=jnp.float32
        ).astype(jnp.bfloat16)
        remote(
            page_send.at[tile], page_recv.at[tile], page_send_sem, page_recv_sem.at[index],
            (blk, mate),
        )
    for tile in tiles:
        page_grad_ref[tile, :] = jnp.dot(
            grads[0, tile, :], query_rows[...], preferred_element_type=jnp.float32
        )
    settle(loss_recv, loss_recv_sem)
    loss_ref[0] = jnp.sum(losses[0] + loss_recv[...]) / jnp.float32(total_queries)
    for index, tile in enumerate(tiles):
        settle(page_recv.at[tile], page_recv_sem.at[index])
        page_grad_ref[tile, :] = page_grad_ref[tile, :] + page_recv[tile, :].astype(jnp.float32)

    sums = [jnp.zeros((piece, width), jnp.float32) for _ in range(2)]
    settle(part_recv.at[blk, pl.ds(0, groups - 1)], part_recv_sem.at[blk])
    for group in range(groups):
        sums[group % 2] = sums[group % 2] + part_recv[blk, group].astype(jnp.float32)
    for step in range(blocks - 1):
        origin = step + jnp.where(step >= blk, 1, 0)
        settle(part_recv.at[origin], part_recv_sem.at[origin])
        for group in range(groups):
            sums[group % 2] = sums[group % 2] + part_recv[origin, group].astype(jnp.float32)
    for index in range(2):
        query_grad_ref[index] = sums[index]
    query_grad_ref[half] = query_grad_ref[half] + own_term[grp]

    settle(held.at[0, pl.ds(0, groups - 1)], column_send)
    settle(held.at[pl.ds(0, blocks - 1)], row_send)
    settle(count_rows.at[pl.ds(0, blocks - 1)], count_send)
    settle(page_ref.at[1], mate_send.at[0])
    settle(extra_rows, mate_send.at[1])
    settle(part_send.at[0, pl.ds(0, groups - 1)], near_send)
    settle(part_send.at[pl.ds(0, blocks - 1)], far_send)
    settle(page_send, page_send_sem)
    settle(loss_send, loss_send_sem)


def write_out(query_grad_in, page_grad_in, loss_in, query_grad_ref, page_grad_ref, loss_ref, sems):
    copies = [
        pltpu.make_async_copy(page_grad_in, page_grad_ref, sems.at[0]),
        pltpu.make_async_copy(query_grad_in, query_grad_ref, sems.at[1]),
        pltpu.make_async_copy(loss_in, loss_ref, sems.at[2]),
    ]
    for copy in copies:
        copy.start()
    for copy in copies:
        copy.wait()


def local(queries, token_counts, pages, patch_counts, labels):
    blocks = lax.axis_size("blk")
    groups = lax.axis_size("grp")
    block_queries, slice_tokens, width = queries.shape
    patches = pages.shape[1]
    half_queries = block_queries // 2
    piece = half_queries * slice_tokens
    rows = piece * groups
    vmem = pl.BlockSpec(memory_space=pltpu.VMEM)
    smem = pl.BlockSpec(memory_space=pltpu.SMEM)
    anywhere = pl.BlockSpec(memory_space=pl.ANY)
    dma = pltpu.SemaphoreType.DMA
    f32, bf16 = jnp.float32, jnp.bfloat16
    query_grad, page_grad, page_loss = pl.pallas_call(
        functools.partial(kernel, blocks, groups, half_queries, slice_tokens),
        out_shape=(
            pltpu.VMEM((2, piece, width), f32),
            pltpu.VMEM((patches, width), f32),
            pltpu.SMEM((1,), f32),
        ),
        in_specs=[anywhere] * 5,
        out_specs=(vmem, vmem, smem),
        scratch_shapes=[
            pltpu.SMEM(token_counts.shape, jnp.int32),
            pltpu.VMEM((2, patches, width), bf16),
            pltpu.VMEM((2, width, patches), bf16),
            pltpu.SMEM((1,), jnp.int32),
            pltpu.SMEM((1, labels.shape[0]), jnp.int32),
            pltpu.VMEM((blocks, groups, piece, width), bf16),
            pltpu.VMEM((blocks * rows, width), bf16),
            pltpu.VMEM((blocks, 1, rows), f32),
            pltpu.VMEM((2, blocks + 1, 1, rows), f32),
            pltpu.VMEM((blocks + 1, 1, rows), f32),
            pltpu.VMEM((2, patches - patches // 2, rows), f32),
            pltpu.VMEM((2, patches // 8, 8, rows), f32),
            pltpu.VMEM((2, patches // 8, 8, rows), f32),
            pltpu.VMEM((2, patches, blocks * rows), bf16),
            pltpu.VMEM((groups, piece, width), f32),
            pltpu.VMEM((blocks, groups, piece, width), bf16),
            pltpu.VMEM((blocks, groups, piece, width), bf16),
            pltpu.VMEM((patches, width), bf16),
            pltpu.VMEM((patches, width), bf16),
            pltpu.VMEM((1, rows), f32),
            pltpu.VMEM((1, rows), f32),
            dma, dma((groups,)), dma, dma((blocks,)), dma, dma((blocks,)),
            dma((2,)), dma((2,)), dma, dma, dma((blocks,)),
            dma, dma((patches // patch_tile,)), dma, dma, dma((5,)),
        ],
        compiler_params=pltpu.CompilerParams(
            collective_id=0, has_side_effects=True, vmem_limit_bytes=60 * 1024 * 1024
        ),
        name="late_interaction",
    )(queries.reshape(2, piece, width), token_counts, pages[0], patch_counts, labels.T)
    query_grad, page_grad, page_loss = pl.pallas_call(
        write_out,
        out_shape=(
            jax.ShapeDtypeStruct((2, piece, width), f32),
            jax.ShapeDtypeStruct((patches, width), f32),
            jax.ShapeDtypeStruct((1,), f32),
        ),
        in_specs=[anywhere] * 3,
        out_specs=(anywhere,) * 3,
        scratch_shapes=[dma((3,))],
        compiler_params=pltpu.CompilerParams(vmem_limit_bytes=1024 * 1024),
        name="write_out",
    )(query_grad, page_grad, page_loss)
    return query_grad.reshape(queries.shape), page_grad[None], page_loss


def solution(mesh):
    in_specs = (
        P("blk", "grp", None),
        P("blk"),
        P(("blk", "grp"), None, None),
        P(("blk", "grp")),
        P(None, ("blk", "grp")),
    )
    out_specs = (P("blk", "grp", None), P(("blk", "grp"), None, None), P(("blk", "grp")))
    return jax.shard_map(local, mesh=mesh, in_specs=in_specs, out_specs=out_specs, check_vma=False)
```

time: 26 us -> 20.9 us (0.80)
  the two profiles are of different devices: /device:TPU:0 before, /device:TPU:7 now
where the time goes in v1:
time: 20.9 us; the launch traced here: 20.7 us
  Pallas kernels  19.4 us (93%)
  between operations  1.29 us (6%)
    pallas_call x1, Pallas kernels, local(): pl.pallas_call(functools.partial(kernel, blocks, groups, half_queries, sl...  18.6 us
    pallas_call x1, Pallas kernels, local(): pl.pallas_call(write_out, out_shape=(jax.ShapeDtypeStruct((2, piece, widt...  0.83 us

profile of v1, /device:TPU:7, one launch (start us, length us, event | category | flops | bytes accessed | tf_op | source)
XLA Modules:
  0.0 20.7 jit_solution(7703312155509755378)
XLA Ops:
  1.3 18.6 %late_interaction.1 = (f32[2,16,128]{2,1,0:T(8,128)S(1)}, f32[1024,128]{1,0:T(8,128)S(1)}, f32[1]{0:T(128)S(4)}) custom-call(bf16[2,16,128]{2,1,0:T(8,128)(2,1)} %bitcast.6, s32[8]{0:T(128)} %count_in.1, bf16[1024,128]{1,0:T(8,128)(2,1)} %bitcast.5, s32[1]{0:T(128)S(6)} %copy.8.patch_count_in, s32[1,32]{1,0:T(1,128)} %bitcast.7), custom_call_target="tpu_custom_call" | custom-call | tf_op jit(solution)/shard_map/late_interaction/pallas_call | solution.py:343
  19.9 0.8 %write_out.1 = (f32[2,16,128]{2,1,0:T(8,128)}, f32[1024,128]{1,0:T(8,128)}, f32[1]{0:T(128)}) custom-call(f32[2,16,128]{2,1,0:T(8,128)S(1)} %get-tuple-element.9.query_grad_in, f32[1024,128]{1,0:T(8,128)S(1)} %get-tuple-element.10.page_grad_in, f32[1]{0:T(128)S(4)} %get-tuple-element.11.loss_in), custom_call_target="tpu_custom_call" | custom-call | tf_op jit(solution)/shard_map/write_out/pallas_call | solution.py:383

commit v2 on v1

v2 whole, which is shorter than its diff:
```python
import functools
import math

import jax
import jax.numpy as jnp
from jax import lax
from jax.experimental import pallas as pl
from jax.experimental.pallas import tpu as pltpu
from jax.sharding import PartitionSpec as P

align_sharpness = 4.0
logit_scale = 2.0
logit_bias = -5.0
masked = -1e30
exp2_scale = align_sharpness * math.log2(math.e)
MESH = pl.DeviceIdType.MESH
patch_tile = 256


def partner(position, step, size):
    if size & (size - 1):
        return lax.rem(position + step, size)
    result = 0
    bit = 1
    while bit < size:
        here = lax.rem(position // bit, 2)
        flip = (step // bit) % 2
        result = result + (1 - here if flip else here) * bit
        bit *= 2
    return result


def source(position, step, size):
    if size & (size - 1):
        return lax.rem(position + size - step, size)
    return partner(position, step, size)


def fold(value):
    return value.reshape(-1, 8, value.shape[1])


def kernel(
    blocks, groups, half_queries, slice_tokens,
    query_in, count_in, page_in, patch_count_in, label_in,
    query_grad_ref, page_grad_ref, loss_ref,
    query_ref, count_ref, page_ref, page_turned, patch_count_ref, label_ref,
    held, query_rows, count_rows, label_rows, extra_rows, bias,
    score_ref, shifted_ref, exponent_ref, grads, own_term,
    part_send, part_recv, page_send, page_recv, loss_send, loss_recv,
    column_send, column_recv, row_send, row_recv, count_send, count_recv,
    relay_send, row_ready, column_ready, mate_send, mate_recv, near_send, far_send, part_recv_sem,
    page_send_sem, page_recv_sem, loss_send_sem, loss_recv_sem, load_sem,
):
    blk = lax.axis_index("blk")
    grp = lax.axis_index("grp")
    half = lax.rem(grp, 2)
    mate = grp + 1 - 2 * half
    patches, width = page_in.shape
    piece = half_queries * slice_tokens
    rows = piece * groups
    free = patches // 2
    total_queries = blocks * half_queries * 2
    tiles = [pl.ds(start, patch_tile) for start in range(0, patches, patch_tile)]
    tile_folds = patch_tile // 8
    slot = jnp.minimum(grp, 0)
    spans = [pl.ds(start, patches // 2) for start in (0, patches // 2)]
    mine, theirs = pl.ds(0, width), pl.ds(width, width)

    chip = grp // 2
    chips = groups // 2
    barrier = pltpu.get_barrier_semaphore()

    def greet(sem, device):
        pl.semaphore_signal(sem, inc=1, device_id=device, device_id_type=MESH)

    for step in range(1, groups):
        target = partner(grp, step, groups)
        pl.when(target // 2 >= chip - 1)(
            functools.partial(greet, barrier, (blk, target))
        )
    for step in range(1, blocks):
        target = partner(blk, step, blocks)
        pl.when(target > blk)(functools.partial(greet, barrier, (target, grp)))

    loads = [
        pltpu.make_async_copy(src, dst, load_sem.at[index])
        for index, (src, dst) in enumerate((
            (count_in, count_ref), (label_in, label_ref), (patch_count_in, patch_count_ref),
            (query_in, query_ref), (page_in, page_ref.at[:, mine]),
        ))
    ]
    for index in (3, 0, 1, 2, 4):
        loads[index].start()

    def remote(src, dst, send, recv, device):
        pltpu.make_async_remote_copy(
            src_ref=src, dst_ref=dst, send_sem=send, recv_sem=recv,
            device_id=device, device_id_type=MESH,
        ).start()

    def settle(ref, sem):
        pltpu.make_async_copy(ref, ref, sem).wait()

    def give_piece(target):
        remote(
            query_ref.at[lax.rem(target, 2)], held.at[blk, grp], column_send, column_recv.at[chip],
            (blk, target),
        )

    pl.semaphore_wait(barrier, 1 + 2 * chip + 2 * jnp.where(chip + 1 < chips, 1, 0) + blk)
    for step in range(1, blocks):
        target = partner(blk, step, blocks)
        pl.when(target < blk)(functools.partial(greet, row_ready, (target, grp)))
    for step in range(1, groups):
        target = partner(grp, step, groups)
        pl.when((target // 2 <= chip - 2) & (target >= 2))(
            functools.partial(greet, column_ready, (blk, target))
        )
    loads[3].wait()
    for step in range(1, groups):
        target = partner(grp, step, groups)
        pl.when(target // 2 <= chip + 1)(functools.partial(give_piece, target))
    held[blk, grp] = query_ref[half]
    remote(page_in, page_ref.at[:, theirs], mate_send.at[0], mate_recv.at[0], (blk, mate))

    @pl.when((chip > 0) & (chip + 2 < chips))
    def _():
        pl.semaphore_wait(column_ready, 2 * (chips - 2 - chip))
        for step in range(1, groups):
            target = partner(grp, step, groups)
            pl.when(target // 2 > chip + 1)(functools.partial(give_piece, target))

    @pl.when(chip == 1)
    def _():
        pair = held.at[blk, pl.ds(0, 2)]
        settle(pair, column_recv.at[0])
        for target in range(chips - 1, 1, -1):
            remote(pair, pair, relay_send, column_recv.at[0], (blk, 2 * target + half))

    @pl.when(blk + 1 < blocks)
    def _():
        pl.semaphore_wait(row_ready, blocks - 1 - blk)

    for step in range(blocks - 1, 0, -1):
        other = partner(blk, step, blocks)
        remote(query_ref.at[half], held.at[blk, grp], row_send, row_recv.at[blk], (other, grp))

    lane = lax.broadcasted_iota(jnp.int32, (1, rows), 1)
    query_row = lax.rem(lane // slice_tokens, half_queries)
    token_row = lane // piece * slice_tokens + lax.rem(lane, slice_tokens)

    def spread(read):
        result = jnp.zeros((1, rows), jnp.float32)
        for index in range(half_queries):
            result = jnp.where(query_row == index, read(index).astype(jnp.float32), result)
        return result

    for load in loads[:3]:
        load.wait()
    count_rows[blk] = spread(lambda index: count_ref[half * half_queries + index])
    for index in range(blocks):
        first = index * half_queries * 2
        label_rows[0, index] = spread(
            lambda query: label_ref[0, first + half * half_queries + query]
        )
        extra_rows[index] = spread(
            lambda query: label_ref[0, first + (1 - half) * half_queries + query]
        )
    patch_count = patch_count_ref[0].astype(jnp.float32)
    extra_rows[blocks] = jnp.full((1, rows), patch_count, jnp.float32)
    for step in range(blocks - 1, 0, -1):
        other = partner(blk, step, blocks)
        remote(count_rows.at[blk], count_rows.at[blk], count_send, count_recv, (other, grp))
    remote(extra_rows, label_rows.at[1], mate_send.at[1], mate_recv.at[1], (blk, mate))

    patch = (free + lax.broadcasted_iota(jnp.int32, (patches - free, rows), 0)).astype(jnp.float32)
    same_query = (
        lax.rem(lax.broadcasted_iota(jnp.int32, (rows, rows), 0) // slice_tokens, half_queries)
        == lax.rem(lax.broadcasted_iota(jnp.int32, (rows, rows), 1) // slice_tokens, half_queries)
    )
    same_query = jnp.where(same_query, 1.0, 0.0).astype(jnp.bfloat16)
    loads[4].wait()
    bias[:, pl.ds(0, rows)] = jnp.where(patch < patch_count, 0.0, masked)
    page_turned[mine, :] = page_ref[:, mine].T
    part_recv[blk, grp] = jnp.zeros((piece, width), part_recv.dtype)

    def forward(start, size):
        for hop in range(blocks - 1, 0, -1):
            remote(
                held.at[blk, pl.ds(start, size)], held.at[blk, pl.ds(start, size)], row_send,
                row_recv.at[blk], (partner(blk, hop, blocks), grp),
            )

    settle(held.at[blk, mate], column_recv.at[chip])
    forward(mate, 1)
    for step in range(1, chips):
        other = source(chip, step, chips)
        with jax.named_scope("w_col%d" % step):
            pl.when((chip != 1) | (other >= 1))(functools.partial(
                settle, held.at[blk, pl.ds(2 * other, 2)], column_recv.at[other]
            ))

        forward(2 * other, 2)

    settle(page_ref.at[:, theirs], mate_recv.at[0])
    settle(label_rows.at[1], mate_recv.at[1])
    bias[:, pl.ds(rows, rows)] = jnp.where(patch < label_rows[1, blocks], 0.0, masked)
    page_turned[theirs, :] = page_ref[:, theirs].T

    def both(value):
        return jnp.concatenate([value, value], axis=1)

    token_rows = both(token_row)

    def score_pass(query_pair):
        top = None
        for span in spans:
            scores = lax.dot_general(
                page_ref[span, :], query_pair, (((1,), (1,)), ((), ())),
                preferred_element_type=jnp.float32,
            )
            for start in range(0, span.size, patch_tile):
                part = scores[start:start + patch_tile]
                first = span.start + start
                if first >= free:
                    part = part + bias[pl.ds(first - free, patch_tile), :]
                part = fold(part)
                score_ref[0, pl.ds(first // 8, tile_folds)] = part
                part_top = jnp.max(part, axis=0)
                top = part_top if top is None else jnp.maximum(top, part_top)
        return top

    def exponent_pass(top):
        total = jnp.zeros((8, 2 * rows), jnp.float32)
        moment = jnp.zeros((8, 2 * rows), jnp.float32)
        span = patches // 8 // 2

        def body(index, carry):
            place = pl.ds(index * span, span)
            shifted = score_ref[0, place] - top
            exponent = jnp.exp2(shifted * exp2_scale)
            shifted_ref[0, place] = shifted
            exponent_ref[0, place] = exponent
            return (
                carry[0] + jnp.sum(exponent, axis=0), carry[1] + jnp.sum(exponent * shifted, axis=0)
            )

        return lax.fori_loop(0, 2, body, (total, moment))

    def pair_terms(top, total, moment, origin):
        row_max = jnp.max(top, axis=0, keepdims=True)
        gap = top - row_max
        scale = jnp.exp2(gap * exp2_scale)
        moment = scale * (moment + gap * total)
        total = jnp.sum(scale * total, axis=0, keepdims=True)
        shifted_score = jnp.sum(moment, axis=0, keepdims=True) / total
        token_score = shifted_score + row_max

        count_row = both(count_rows[origin])
        live = token_rows.astype(jnp.float32) < count_row
        live_score = jnp.where(live, token_score, 0.0)
        sublane = lax.broadcasted_iota(jnp.int32, (16, rows), 0)
        pieces = jnp.zeros((16, rows), jnp.float32)
        for page in range(2):
            remaining = live_score[:, page * rows:(page + 1) * rows]
            for index in range(3):
                value = remaining.astype(jnp.bfloat16).astype(jnp.float32)
                pieces = jnp.where(sublane == 8 * page + index, value, pieces)
                remaining = remaining - value
        piece_sums = jnp.dot(
            pieces.astype(jnp.bfloat16), same_query, preferred_element_type=jnp.float32
        )
        pair_sum = jnp.concatenate(
            [jnp.sum(piece_sums[8 * page:8 * page + 8], axis=0, keepdims=True) for page in range(2)],
            axis=1,
        )
        pair_score = pair_sum / count_row
        labels = jnp.concatenate([label_rows[0, origin], label_rows[1, origin]], axis=1)
        label_sign = 2.0 * labels - 1.0
        signed = -label_sign * (logit_scale * pair_score + logit_bias)
        decay = jnp.exp(-jnp.abs(signed))
        softplus = jnp.maximum(signed, 0.0) + jnp.log1p(decay)
        sigmoid = jnp.where(signed >= 0.0, 1.0, decay) / (1.0 + decay)
        loss_row = jnp.where(token_rows == 0, softplus, 0.0)
        token_grad = jnp.where(live, -label_sign * logit_scale * sigmoid / count_row, 0.0) / total
        slope = scale * token_grad
        offset = slope * (1.0 + align_sharpness * (gap - shifted_score))
        return offset, slope * align_sharpness, loss_row

    def block_terms(order, origin):
        queries = held[origin].reshape(rows, width)
        empty = jnp.zeros((rows, width), jnp.bfloat16)
        query_pair = jnp.concatenate([
            jnp.concatenate([queries, empty], axis=1), jnp.concatenate([empty, queries], axis=1)
        ], axis=0)
        columns = pl.ds(order * 2 * rows, 2 * rows)
        query_rows[columns, :] = query_pair
        top = score_pass(query_pair)
        offset, slope, loss_row = pair_terms(top, *exponent_pass(top), origin)
        for index, tile in enumerate(tiles):
            place = pl.ds(index * tile_folds, tile_folds)
            tile_grad = exponent_ref[slot, place] * (offset + slope * shifted_ref[slot, place])
            grads[tile, columns] = tile_grad.reshape(patch_tile, 2 * rows).astype(jnp.bfloat16)
        query_term = jnp.zeros((width, rows), jnp.float32)
        for span in spans:
            terms = jnp.dot(
                page_turned[:, span], grads[span, columns], preferred_element_type=jnp.float32
            )
            query_term = query_term + terms[:width, :rows] + terms[width:, rows:]
        return query_term.T, loss_row

    own, losses = block_terms(0, blk)
    own_term[...] = own.reshape(groups, piece, width)
    part_send[blk] = own.astype(jnp.bfloat16).reshape(groups, piece, width)
    for step in range(groups - 1, 0, -1):
        target = partner(grp, step, groups)
        remote(
            part_send.at[blk, target], part_recv.at[blk, grp], near_send, part_recv_sem.at[blk],
            (blk, target),
        )

    for step in range(blocks - 1):
        origin = step + jnp.where(step >= blk, 1, 0)
        settle(held.at[origin], row_recv.at[origin])
        if step == 0:
            settle(count_rows.at[pl.ds(0, blocks - 1)], count_recv)
        query_term, block_losses = block_terms(step + 1, origin)
        losses = losses + block_losses
        part_send[origin] = query_term.astype(jnp.bfloat16).reshape(groups, piece, width)
        for target in range(groups):
            remote(
                part_send.at[origin, target], part_recv.at[blk, grp], far_send,
                part_recv_sem.at[blk], (origin, target),
            )

    loss_send[...] = losses[:, rows:]
    remote(loss_send, loss_recv, loss_send_sem, loss_recv_sem, (blk, mate))
    for span in spans:
        page_terms = jnp.dot(grads[span, :], query_rows[...], preferred_element_type=jnp.float32)
        page_send[span, :] = page_terms[:, width:].astype(jnp.bfloat16)
        page_grad_ref[span, :] = page_terms[:, :width]
        remote(
            page_send.at[span], page_recv.at[span], page_send_sem, page_recv_sem,
            (blk, mate),
        )
    settle(loss_recv, loss_recv_sem)
    loss_ref[0] = jnp.sum(losses[:, :rows] + loss_recv[...]) / jnp.float32(total_queries)
    settle(page_recv, page_recv_sem)
    page_grad_ref[...] = page_grad_ref[...] + page_recv[...].astype(jnp.float32)

    @pl.when(chip > 0)
    def _():
        settle(held.at[0, pl.ds(0, groups - 1)], column_send)

    @pl.when(chip == 0)
    def _():
        settle(held.at[0, pl.ds(0, 3)], column_send)

    @pl.when(chip == 1)
    def _():
        settle(held.at[0, pl.ds(0, 2 * (chips - 2))], relay_send)

    settle(held.at[pl.ds(0, blocks - 1)], row_send)
    settle(count_rows.at[pl.ds(0, blocks - 1)], count_send)
    settle(page_ref.at[:, theirs], mate_send.at[0])
    settle(extra_rows, mate_send.at[1])
    settle(part_send.at[0, pl.ds(0, groups - 1)], near_send)
    settle(part_send.at[pl.ds(0, blocks - 1)], far_send)
    settle(page_send, page_send_sem)
    settle(loss_send, loss_send_sem)

    sums = [jnp.zeros((piece, width), jnp.float32) for _ in range(2)]
    settle(part_recv.at[blk, pl.ds(0, groups - 1)], part_recv_sem.at[blk])
    for group in range(groups):
        sums[group % 2] = sums[group % 2] + part_recv[blk, group].astype(jnp.float32)
    for step in range(blocks - 1):
        origin = step + jnp.where(step >= blk, 1, 0)
        settle(part_recv.at[origin], part_recv_sem.at[origin])
        for group in range(groups):
            sums[group % 2] = sums[group % 2] + part_recv[origin, group].astype(jnp.float32)
    for index in range(2):
        query_grad_ref[index] = sums[index]
    query_grad_ref[half] = query_grad_ref[half] + own_term[grp]


def write_out(query_grad_in, page_grad_in, loss_in, query_grad_ref, page_grad_ref, loss_ref, sems):
    copies = [
        pltpu.make_async_copy(page_grad_in, page_grad_ref, sems.at[0]),
        pltpu.make_async_copy(query_grad_in, query_grad_ref, sems.at[1]),
        pltpu.make_async_copy(loss_in, loss_ref, sems.at[2]),
    ]
    for copy in copies:
        copy.start()
    for copy in copies:
        copy.wait()


def local(queries, token_counts, pages, patch_counts, labels):
    blocks = lax.axis_size("blk")
    groups = lax.axis_size("grp")
    block_queries, slice_tokens, width = queries.shape
    patches = pages.shape[1]
    half_queries = block_queries // 2
    piece = half_queries * slice_tokens
    rows = piece * groups
    vmem = pl.BlockSpec(memory_space=pltpu.VMEM)
    smem = pl.BlockSpec(memory_space=pltpu.SMEM)
    anywhere = pl.BlockSpec(memory_space=pl.ANY)
    dma = pltpu.SemaphoreType.DMA
    f32, bf16 = jnp.float32, jnp.bfloat16
    query_grad, page_grad, page_loss = pl.pallas_call(
        functools.partial(kernel, blocks, groups, half_queries, slice_tokens),
        out_shape=(
            pltpu.VMEM((2, piece, width), f32),
            pltpu.VMEM((patches, width), f32),
            pltpu.SMEM((1,), f32),
        ),
        in_specs=[anywhere] * 5,
        out_specs=(vmem, vmem, smem),
        scratch_shapes=[
            pltpu.VMEM((2, piece, width), bf16),
            pltpu.SMEM(token_counts.shape, jnp.int32),
            pltpu.VMEM((patches, 2 * width), bf16),
            pltpu.VMEM((2 * width, patches), bf16),
            pltpu.SMEM((1,), jnp.int32),
            pltpu.SMEM((1, labels.shape[0]), jnp.int32),
            pltpu.VMEM((blocks, groups, piece, width), bf16),
            pltpu.VMEM((blocks * 2 * rows, 2 * width), bf16),
            pltpu.VMEM((blocks, 1, rows), f32),
            pltpu.VMEM((2, blocks + 1, 1, rows), f32),
            pltpu.VMEM((blocks + 1, 1, rows), f32),
            pltpu.VMEM((patches - patches // 2, 2 * rows), f32),
            pltpu.VMEM((1, patches // 8, 8, 2 * rows), f32),
            pltpu.VMEM((1, patches // 8, 8, 2 * rows), f32),
            pltpu.VMEM((1, patches // 8, 8, 2 * rows), f32),
            pltpu.VMEM((patches, blocks * 2 * rows), bf16),
            pltpu.VMEM((groups, piece, width), f32),
            pltpu.VMEM((blocks, groups, piece, width), bf16),
            pltpu.VMEM((blocks, groups, piece, width), bf16),
            pltpu.VMEM((patches, width), bf16),
            pltpu.VMEM((patches, width), bf16),
            pltpu.VMEM((1, rows), f32),
            pltpu.VMEM((1, rows), f32),
            dma, dma((groups // 2,)), dma, dma((blocks,)), dma, dma,
            dma, pltpu.SemaphoreType.REGULAR, pltpu.SemaphoreType.REGULAR,
            dma((2,)), dma((2,)), dma, dma, dma((blocks,)),
            dma, dma, dma, dma, dma((5,)),
        ],
        compiler_params=pltpu.CompilerParams(
            collective_id=0, has_side_effects=True, vmem_limit_bytes=60 * 1024 * 1024
        ),
        name="late_interaction",
    )(queries.reshape(2, piece, width), token_counts, pages[0], patch_counts, labels.T)
    query_grad, page_grad, page_loss = pl.pallas_call(
        write_out,
        out_shape=(
            jax.ShapeDtypeStruct((2, piece, width), f32),
            jax.ShapeDtypeStruct((patches, width), f32),
            jax.ShapeDtypeStruct((1,), f32),
        ),
        in_specs=[anywhere] * 3,
        out_specs=(anywhere,) * 3,
        scratch_shapes=[dma((3,))],
        compiler_params=pltpu.CompilerParams(vmem_limit_bytes=1024 * 1024),
        name="write_out",
    )(query_grad, page_grad, page_loss)
    return query_grad.reshape(queries.shape), page_grad[None], page_loss


def solution(mesh):
    in_specs = (
        P("blk", "grp", None),
        P("blk"),
        P(("blk", "grp"), None, None),
        P(("blk", "grp")),
        P(None, ("blk", "grp")),
    )
    out_specs = (P("blk", "grp", None), P(("blk", "grp"), None, None), P(("blk", "grp")))
    return jax.shard_map(local, mesh=mesh, in_specs=in_specs, out_specs=out_specs, check_vma=False)
```

time: 20.9 us -> 20.5 us (0.981)
  Pallas kernels: 19.4 us -> 19 us
    pallas_call x1, Pallas kernels: 18.6 us -> 18.2 us  [local(): pl.pallas_call(functools.partial(kernel, blocks, groups, half_queries, sl...]
where the time goes in v2:
time: 20.5 us; the launch traced here: 20.3 us
  Pallas kernels  19 us (93%)
  between operations  1.29 us (6%)
    pallas_call x1, Pallas kernels, local(): pl.pallas_call(functools.partial(kernel, blocks, groups, half_queries, sl...  18.2 us
    pallas_call x1, Pallas kernels, local(): pl.pallas_call(write_out, out_shape=(jax.ShapeDtypeStruct((2, piece, widt...  0.83 us

profile of v2, /device:TPU:7, one launch (start us, length us, event | category | flops | bytes accessed | tf_op | source)
XLA Modules:
  0.0 20.3 jit_solution(210586195313665742)
XLA Ops:
  1.3 18.2 %late_interaction.1 = (f32[2,16,128]{2,1,0:T(8,128)S(1)}, f32[1024,128]{1,0:T(8,128)S(1)}, f32[1]{0:T(128)S(4)}) custom-call(bf16[2,16,128]{2,1,0:T(8,128)(2,1)} %bitcast.6, s32[8]{0:T(128)} %count_in.1, bf16[1024,128]{1,0:T(8,128)(2,1)} %bitcast.5, s32[1]{0:T(128)S(6)} %copy.8.patch_count_in, s32[1,32]{1,0:T(1,128)} %bitcast.7), custom_call_target="tpu_custom_call" | custom-call | tf_op jit(solution)/shard_map/late_interaction/pallas_call | solution.py:412
  19.5 0.8 %write_out.1 = (f32[2,16,128]{2,1,0:T(8,128)}, f32[1024,128]{1,0:T(8,128)}, f32[1]{0:T(128)}) custom-call(f32[2,16,128]{2,1,0:T(8,128)S(1)} %get-tuple-element.9.query_grad_in, f32[1024,128]{1,0:T(8,128)S(1)} %get-tuple-element.10.page_grad_in, f32[1]{0:T(128)S(4)} %get-tuple-element.11.loss_in), custom_call_target="tpu_custom_call" | custom-call | tf_op jit(solution)/shard_map/write_out/pallas_call | solution.py:455

commit v3 on v2

--- a/solution.py
+++ b/solution.py
@@ -45,7 +45,7 @@
     query_in, count_in, page_in, patch_count_in, label_in,
     query_grad_ref, page_grad_ref, loss_ref,
     query_ref, count_ref, page_ref, page_turned, patch_count_ref, label_ref,
-    held, query_rows, count_rows, label_rows, extra_rows, bias,
+    held, query_rows, token_grads, count_rows, label_rows, extra_rows, bias,
     score_ref, shifted_ref, exponent_ref, grads, own_term,
     part_send, part_recv, page_send, page_recv, loss_send, loss_recv,
     column_send, column_recv, row_send, row_recv, count_send, count_recv,
@@ -184,6 +184,7 @@
     bias[:, pl.ds(0, rows)] = jnp.where(patch < patch_count, 0.0, masked)
     page_turned[mine, :] = page_ref[:, mine].T
     part_recv[blk, grp] = jnp.zeros((piece, width), part_recv.dtype)
+    query_rows[...] = jnp.zeros_like(query_rows)
 
     def forward(start, size):
         for hop in range(blocks - 1, 0, -1):
@@ -283,10 +284,10 @@
         softplus = jnp.maximum(signed, 0.0) + jnp.log1p(decay)
         sigmoid = jnp.where(signed >= 0.0, 1.0, decay) / (1.0 + decay)
         loss_row = jnp.where(token_rows == 0, softplus, 0.0)
-        token_grad = jnp.where(live, -label_sign * logit_scale * sigmoid / count_row, 0.0) / total
-        slope = scale * token_grad
+        token_grad = jnp.where(live, -label_sign * logit_scale * sigmoid / count_row, 0.0)
+        slope = scale / total
         offset = slope * (1.0 + align_sharpness * (gap - shifted_score))
-        return offset, slope * align_sharpness, loss_row
+        return offset, slope * align_sharpness, token_grad, loss_row
 
     def block_terms(order, origin):
         queries = held[origin].reshape(rows, width)
@@ -295,9 +296,9 @@
             jnp.concatenate([queries, empty], axis=1), jnp.concatenate([empty, queries], axis=1)
         ], axis=0)
         columns = pl.ds(order * 2 * rows, 2 * rows)
-        query_rows[columns, :] = query_pair
         top = score_pass(query_pair)
-        offset, slope, loss_row = pair_terms(top, *exponent_pass(top), origin)
+        offset, slope, token_grad, loss_row = pair_terms(top, *exponent_pass(top), origin)
+        token_grads[order] = token_grad
         for index, tile in enumerate(tiles):
             place = pl.ds(index * tile_folds, tile_folds)
             tile_grad = exponent_ref[slot, place] * (offset + slope * shifted_ref[slot, place])
@@ -307,7 +308,9 @@
             terms = jnp.dot(
                 page_turned[:, span], grads[span, columns], preferred_element_type=jnp.float32
             )
-            query_term = query_term + terms[:width, :rows] + terms[width:, rows:]
+            query_term = query_term + (
+                terms[:width, :rows] * token_grad[:, :rows] + terms[width:, rows:] * token_grad[:, rows:]
+            )
         return query_term.T, loss_row
 
     own, losses = block_terms(0, blk)
@@ -336,6 +339,23 @@
 
     loss_send[...] = losses[:, rows:]
     remote(loss_send, loss_recv, loss_send_sem, loss_recv_sem, (blk, mate))
+    same_row = (
+        lax.broadcasted_iota(jnp.int32, (rows, rows), 0)
+        == lax.broadcasted_iota(jnp.int32, (rows, rows), 1)
+    )
+    for order in range(blocks):
+        origin = blk if order == 0 else order - 1 + jnp.where(order - 1 >= blk, 1, 0)
+        queries = held[origin].reshape(rows, width)
+        for page in range(2):
+            spread_grad = jnp.where(same_row, token_grads[order, :, page * rows:(page + 1) * rows], 0.0)
+            high = spread_grad.astype(jnp.bfloat16)
+            low = (spread_grad - high.astype(jnp.float32)).astype(jnp.bfloat16)
+            query_rows[
+                pl.ds((order * 2 + page) * rows, rows), pl.ds(page * width, width)
+            ] = jnp.dot(
+                jnp.concatenate([high, low], axis=1), jnp.concatenate([queries, queries], axis=0),
+                preferred_element_type=jnp.float32,
+            ).astype(jnp.bfloat16)
     for span in spans:
         page_terms = jnp.dot(grads[span, :], query_rows[...], preferred_element_type=jnp.float32)
         page_send[span, :] = page_terms[:, width:].astype(jnp.bfloat16)
@@ -427,6 +447,7 @@
             pltpu.SMEM((1, labels.shape[0]), jnp.int32),
             pltpu.VMEM((blocks, groups, piece, width), bf16),
             pltpu.VMEM((blocks * 2 * rows, 2 * width), bf16),
+            pltpu.VMEM((blocks, 1, 2 * rows), f32),
             pltpu.VMEM((blocks, 1, rows), f32),
             pltpu.VMEM((2, blocks + 1, 1, rows), f32),
             pltpu.VMEM((blocks + 1, 1, rows), f32),

time: 20.5 us -> 20 us (0.976)
  Pallas kernels: 19 us -> 18.6 us
    pallas_call x1, Pallas kernels: 18.2 us -> 17.8 us  [local(): pl.pallas_call(functools.partial(kernel, blocks, groups, half_queries, sl...]
where the time goes in v3:
time: 20 us; the launch traced here: 19.9 us
  Pallas kernels  18.6 us (93%)
  between operations  1.29 us (6%)
    pallas_call x1, Pallas kernels, local(): pl.pallas_call(functools.partial(kernel, blocks, groups, half_queries, sl...  17.8 us
    pallas_call x1, Pallas kernels, local(): pl.pallas_call(write_out, out_shape=(jax.ShapeDtypeStruct((2, piece, widt...  0.83 us

profile of v3, /device:TPU:7, one launch (start us, length us, event | category | flops | bytes accessed | tf_op | source)
XLA Modules:
  0.0 19.9 jit_solution(3655870957797783669)
XLA Ops:
  1.3 17.8 %late_interaction.1 = (f32[2,16,128]{2,1,0:T(8,128)S(1)}, f32[1024,128]{1,0:T(8,128)S(1)}, f32[1]{0:T(128)S(4)}) custom-call(bf16[2,16,128]{2,1,0:T(8,128)(2,1)} %bitcast.6, s32[8]{0:T(128)} %count_in.1, bf16[1024,128]{1,0:T(8,128)(2,1)} %bitcast.5, s32[1]{0:T(128)S(6)} %copy.8.patch_count_in, s32[1,32]{1,0:T(1,128)} %bitcast.7), custom_call_target="tpu_custom_call" | custom-call | tf_op jit(solution)/shard_map/late_interaction/pallas_call | solution.py:432
  19.0 0.8 %write_out.1 = (f32[2,16,128]{2,1,0:T(8,128)}, f32[1024,128]{1,0:T(8,128)}, f32[1]{0:T(128)}) custom-call(f32[2,16,128]{2,1,0:T(8,128)S(1)} %get-tuple-element.9.query_grad_in, f32[1024,128]{1,0:T(8,128)S(1)} %get-tuple-element.10.page_grad_in, f32[1]{0:T(128)S(4)} %get-tuple-element.11.loss_in), custom_call_target="tpu_custom_call" | custom-call | tf_op jit(solution)/shard_map/write_out/pallas_call | solution.py:476

commit v4 on v3

--- a/solution.py
+++ b/solution.py
@@ -319,7 +319,7 @@
     for step in range(groups - 1, 0, -1):
         target = partner(grp, step, groups)
         remote(
-            part_send.at[blk, target], part_recv.at[blk, grp], near_send, part_recv_sem.at[blk],
+            part_send.at[blk, target], part_recv.at[blk, grp], near_send, part_recv_sem.at[0],
             (blk, target),
         )
 
@@ -334,7 +334,7 @@
         for target in range(groups):
             remote(
                 part_send.at[origin, target], part_recv.at[blk, grp], far_send,
-                part_recv_sem.at[blk], (origin, target),
+                part_recv_sem.at[1], (origin, target),
             )
 
     loss_send[...] = losses[:, rows:]
@@ -391,12 +391,13 @@
     settle(loss_send, loss_send_sem)
 
     sums = [jnp.zeros((piece, width), jnp.float32) for _ in range(2)]
-    settle(part_recv.at[blk, pl.ds(0, groups - 1)], part_recv_sem.at[blk])
+    settle(part_recv.at[blk, pl.ds(0, groups - 1)], part_recv_sem.at[0])
     for group in range(groups):
         sums[group % 2] = sums[group % 2] + part_recv[blk, group].astype(jnp.float32)
     for step in range(blocks - 1):
         origin = step + jnp.where(step >= blk, 1, 0)
-        settle(part_recv.at[origin], part_recv_sem.at[origin])
+        if step == 0:
+            settle(part_recv.at[pl.ds(0, blocks - 1)], part_recv_sem.at[1])
         for group in range(groups):
             sums[group % 2] = sums[group % 2] + part_recv[origin, group].astype(jnp.float32)
     for index in range(2):
@@ -465,7 +466,7 @@
             pltpu.VMEM((1, rows), f32),
             dma, dma((groups // 2,)), dma, dma((blocks,)), dma, dma,
             dma, pltpu.SemaphoreType.REGULAR, pltpu.SemaphoreType.REGULAR,
-            dma((2,)), dma((2,)), dma, dma, dma((blocks,)),
+            dma((2,)), dma((2,)), dma, dma, dma((2,)),
             dma, dma, dma, dma, dma((5,)),
         ],
         compiler_params=pltpu.CompilerParams(

time: 20 us -> 20 us (level)
  no operation moved by 1% of the time
where the time goes in v4:
time: 20 us; the launch traced here: 19.9 us
  Pallas kernels  18.6 us (93%)
  between operations  1.29 us (6%)
    pallas_call x1, Pallas kernels, local(): pl.pallas_call(functools.partial(kernel, blocks, groups, half_queries, sl...  17.7 us
    pallas_call x1, Pallas kernels, local(): pl.pallas_call(write_out, out_shape=(jax.ShapeDtypeStruct((2, piece, widt...  0.83 us

profile of v4, /device:TPU:7, one launch (start us, length us, event | category | flops | bytes accessed | tf_op | source)
XLA Modules:
  0.0 19.9 jit_solution(4841398041557128892)
XLA Ops:
  1.3 17.7 %late_interaction.1 = (f32[2,16,128]{2,1,0:T(8,128)S(1)}, f32[1024,128]{1,0:T(8,128)S(1)}, f32[1]{0:T(128)S(4)}) custom-call(bf16[2,16,128]{2,1,0:T(8,128)(2,1)} %bitcast.6, s32[8]{0:T(128)} %count_in.1, bf16[1024,128]{1,0:T(8,128)(2,1)} %bitcast.5, s32[1]{0:T(128)S(6)} %copy.8.patch_count_in, s32[1,32]{1,0:T(1,128)} %bitcast.7), custom_call_target="tpu_custom_call" | custom-call | tf_op jit(solution)/shard_map/late_interaction/pallas_call | solution.py:433
  19.0 0.8 %write_out.1 = (f32[2,16,128]{2,1,0:T(8,128)}, f32[1024,128]{1,0:T(8,128)}, f32[1]{0:T(128)}) custom-call(f32[2,16,128]{2,1,0:T(8,128)S(1)} %get-tuple-element.9.query_grad_in, f32[1024,128]{1,0:T(8,128)S(1)} %get-tuple-element.10.page_grad_in, f32[1]{0:T(128)S(4)} %get-tuple-element.11.loss_in), custom_call_target="tpu_custom_call" | custom-call | tf_op jit(solution)/shard_map/write_out/pallas_call | solution.py:477

commit v5 on v4

--- a/solution.py
+++ b/solution.py
@@ -304,13 +304,12 @@
             tile_grad = exponent_ref[slot, place] * (offset + slope * shifted_ref[slot, place])
             grads[tile, columns] = tile_grad.reshape(patch_tile, 2 * rows).astype(jnp.bfloat16)
         query_term = jnp.zeros((width, rows), jnp.float32)
-        for span in spans:
+        for page, side in enumerate((mine, theirs)):
             terms = jnp.dot(
-                page_turned[:, span], grads[span, columns], preferred_element_type=jnp.float32
+                page_turned[side, :], grads[:, columns], preferred_element_type=jnp.float32
             )
-            query_term = query_term + (
-                terms[:width, :rows] * token_grad[:, :rows] + terms[width:, rows:] * token_grad[:, rows:]
-            )
+            lanes = slice(page * rows, (page + 1) * rows)
+            query_term = query_term + terms[:, lanes] * token_grad[:, lanes]
         return query_term.T, loss_row
 
     own, losses = block_terms(0, blk)

time: 20 us -> 20 us (level)
  no operation moved by 1% of the time
where the time goes in v5:
time: 20 us; the launch traced here: 19.9 us
  Pallas kernels  18.6 us (93%)
  between operations  1.29 us (6%)
    pallas_call x1, Pallas kernels, local(): pl.pallas_call(functools.partial(kernel, blocks, groups, half_queries, sl...  17.7 us
    pallas_call x1, Pallas kernels, local(): pl.pallas_call(write_out, out_shape=(jax.ShapeDtypeStruct((2, piece, widt...  0.83 us

profile of v5, /device:TPU:7, one launch (start us, length us, event | category | flops | bytes accessed | tf_op | source)
XLA Modules:
  0.0 19.9 jit_solution(1190493034390439382)
XLA Ops:
  1.3 17.7 %late_interaction.1 = (f32[2,16,128]{2,1,0:T(8,128)S(1)}, f32[1024,128]{1,0:T(8,128)S(1)}, f32[1]{0:T(128)S(4)}) custom-call(bf16[2,16,128]{2,1,0:T(8,128)(2,1)} %bitcast.6, s32[8]{0:T(128)} %count_in.1, bf16[1024,128]{1,0:T(8,128)(2,1)} %bitcast.5, s32[1]{0:T(128)S(6)} %copy.8.patch_count_in, s32[1,32]{1,0:T(1,128)} %bitcast.7), custom_call_target="tpu_custom_call" | custom-call | tf_op jit(solution)/shard_map/late_interaction/pallas_call | solution.py:432
  19.0 0.8 %write_out.1 = (f32[2,16,128]{2,1,0:T(8,128)}, f32[1024,128]{1,0:T(8,128)}, f32[1]{0:T(128)}) custom-call(f32[2,16,128]{2,1,0:T(8,128)S(1)} %get-tuple-element.9.query_grad_in, f32[1024,128]{1,0:T(8,128)S(1)} %get-tuple-element.10.page_grad_in, f32[1]{0:T(128)S(4)} %get-tuple-element.11.loss_in), custom_call_target="tpu_custom_call" | custom-call | tf_op jit(solution)/shard_map/write_out/pallas_call | solution.py:476
